TPU v7x, 32 devices: a whole 2x2x4 slice. The times are simulated.
32 devices in a mesh: dp: 8 (over y, x, core), mp: 4 (over z).
Axes of the slice: x: 2, y: 2, z: 4, core: 2. Of those that a mesh axis runs over, the one named last changes fastest.
Arguments:
- layer_input: bfloat16 [32, 8192], P('dp'), may hold values from -6 to 6
- pre_act: bfloat16 [32, 8192], P('dp', 'mp'), may hold values from -8 to 8
- hidden_adjoint: bfloat16 [32, 8192], P('dp', 'mp'), may hold values from -6 to 6
- output_adjoint: bfloat16 [32, 8192], P('dp', 'mp'), may hold values from -6 to 6
Outputs:
- precond_in: float32 [8192, 8192], P('dp', 'mp')
- direction_in: float32 [8192, 8192], P('dp', 'mp')
- precond_out: float32 [8192, 8192], P('dp', 'mp')
- direction_out: float32 [8192, 8192], P('dp', 'mp')
- sq_norm: float32 [], replicated
All inputs are finite; a program needn't handle non-finite values.
Results may differ from a plain program's by a relative error of at most 0.0029.
Values may be sent and summed in bfloat16 or wider, within the bound.
A program may use at most 64 MiB of HBM per device.

v0:
```python
import jax
import jax.numpy as jnp
from jax import lax
from jax.sharding import PartitionSpec as P

D = 8192
H = 8192
DAMPING = 0.1
EXPONENT = 0.75


def square_bf(values):
    wide = values.astype(jnp.float32)
    return (wide * wide).astype(jnp.bfloat16)


def accumulate(act_block, sq_block, adj_piece):
    contract = (((0,), (0,)), ((), ()))
    grad_sum = lax.dot_general(act_block, adj_piece, contract, preferred_element_type=jnp.float32)
    square_sum = lax.dot_general(
        sq_block, square_bf(adj_piece), contract, preferred_element_type=jnp.float32
    )
    return (grad_sum, square_sum)


def finish(partial_value, total_rows):
    gradient = partial_value[0] / total_rows
    precond = (partial_value[1] / total_rows + DAMPING) ** EXPONENT
    norm_term = jnp.sum(gradient * gradient / precond)
    return (gradient, precond, norm_term)


def shards(layer_input, pre_act, hidden_adjoint, output_adjoint):
    preact = pre_act.astype(jnp.float32)
    logistic = jax.nn.sigmoid(preact)
    hidden = (preact * logistic).astype(jnp.bfloat16)
    adjoint = (
        hidden_adjoint.astype(jnp.float32) * logistic * (1.0 + preact * (1.0 - logistic))
    ).astype(jnp.bfloat16)
    own_input = lax.all_to_all(layer_input, "dp", split_axis=1, concat_axis=0, tiled=True)
    sq_input = square_bf(own_input)
    total_rows = own_input.shape[0]
    wide_hidden = lax.all_gather(hidden, "mp", axis=1, tiled=True)
    own_hidden = lax.all_to_all(wide_hidden, "dp", split_axis=1, concat_axis=0, tiled=True)
    sq_hidden = square_bf(own_hidden)
    sums_in = accumulate(own_input, sq_input, lax.all_gather(adjoint, "dp", axis=0, tiled=True))
    sums_out = accumulate(
        own_hidden, sq_hidden, lax.all_gather(output_adjoint, "dp", axis=0, tiled=True)
    )
    gradient_in, precond_in, term_in = finish(sums_in, total_rows)
    gradient_out, precond_out, term_out = finish(sums_out, total_rows)
    sq_norm = lax.psum(term_in + term_out, ("dp", "mp"))
    rescale = jnp.sqrt(2.0 * D * H / sq_norm)
    direction_in = gradient_in / precond_in * rescale
    direction_out = gradient_out / precond_out * rescale
    return (precond_in, direction_in, precond_out, direction_out, sq_norm)


def solution(mesh):
    placed = (P("dp", None), P("dp", "mp"), P("dp", "mp"), P("dp", "mp"))
    return jax.shard_map(
        shards,
        mesh=mesh,
        in_specs=placed,
        out_specs=(P("dp", "mp"), P("dp", "mp"), P("dp", "mp"), P("dp", "mp"), P()),
        check_vma=False,
    )
```

profile of v0, /device:TPU:0, one launch (start us, length us, event | category | flops | bytes accessed | tf_op | source)
XLA Modules:
  0.0 133.4 jit_solution(15350232104087235126)
XLA Ops:
  0.6 5.2 %all-to-all-start = ((bf16[4,8,1024]{2,0,1:T(4,128)(2,1)}), bf16[4,8,1024]{2,0,1:T(4,128)(2,1)S(1)}, u32[]{:S(2)}, u32[]{:S(2)}) async-start(bf16[4,8,1024]{2,0,1:T(4,128)(2,1)} %bitcast.22), calls=%async_computation | async-start | bytes 131072 | tf_op jit(solution)/shard_map/all_to_all | solution.py:40
  5.8 0.8 fusion.13
  6.6 14.1 %all_gather.10 = bf16[4,8192]{1,0:T(4,128)(2,1)} all-gather(bf16[4,2048]{1,0:T(4,128)(2,1)S(1)} %get-tuple-element.9), channel_id=1, replica_groups=mesh['dp'=8,'mp'=4] {'mp'}, dimensions={1}, use_global_device_ids=true | all-gather | bytes 81920 | tf_op jit(solution)/shard_map/all_gather | solution.py:43
  20.7 0.0 all-to-all-done
  20.7 4.3 %all-to-all-start.1 = ((bf16[4,8,1024]{2,0,1:T(4,128)(2,1)}), bf16[4,8,1024]{2,0,1:T(4,128)(2,1)S(1)}, u32[]{:S(2)}, u32[]{:S(2)}) async-start(bf16[4,8,1024]{2,0,1:T(4,128)(2,1)} %bitcast.4), calls=%async_computation.1 | async-start | bytes 131072 | tf_op jit(solution)/shard_map/all_to_all | solution.py:44
  25.0 9.7 %all-gather = bf16[8,4,2048]{2,1,0:T(4,128)(2,1)S(1)} all-gather(bf16[1,4,2048]{2,1,0:T(4,128)(2,1)S(1)} %get-tuple-element.10), channel_id=1, replica_groups=mesh['dp'=8,'mp'=4] {'dp'}, dimensions={0}, use_global_device_ids=true | all-gather | bytes 147456 | tf_op jit(solution)/shard_map/all_gather | solution.py:46
  34.7 9.2 %all-gather.1 = bf16[8,4,2048]{2,1,0:T(4,128)(2,1)S(1)} all-gather(bf16[1,4,2048]{2,1,0:T(4,128)(2,1)} %bitcast.23), channel_id=1, replica_groups=mesh['dp'=8,'mp'=4] {'dp'}, dimensions={0}, use_global_device_ids=true | all-gather | bytes 147456 | tf_op jit(solution)/shard_map/all_gather | solution.py:48
  44.0 0.0 all-to-all-done.1
  44.0 1.3 fusion.6
  45.3 0.0 copy-start
  45.3 7.8 %multiply_reduce_fusion = (f32[]{:T(128)}, f32[1024,2048]{1,0:T(8,128)}) fusion(f32[1024,2048]{1,0:T(8,128)S(1)} %fusion.6, bf16[32,1024]{1,0:T(8,128)(2,1)S(1)} %all_to_all.35, bf16[32,2048]{1,0:T(8,128)(2,1)S(1)} %reshape.19), kind=kOutput, calls=%fused_computation.6 | convolution fusion | flops 146800640 | bytes 16973828 | tf_op jit(solution)/shard_map/dot_general | solution.py:19
  53.1 0.0 copy-done
  53.1 1.3 fusion.5
  54.3 0.0 copy-start.1
  54.4 7.7 %fusion.2 = (f32[]{:T(128)}, f32[2048,1024]{0,1:T(8,128)}) fusion(f32[1024,2048]{1,0:T(8,128)S(1)} %fusion.5, bf16[32,2048]{1,0:T(8,128)(2,1)S(1)} %reshape.17, bf16[32,1024]{1,0:T(8,128)(2,1)S(1)} %all_to_all.31), kind=kOutput, calls=%fused_computation.4 | convolution fusion | flops 146800640 | bytes 16973828 | tf_op jit(solution)/shard_map/dot_general | solution.py:19
  62.0 0.0 copy-done.1
  63.3 39.4 %psum.7 = f32[]{:T(128)} all-reduce(f32[]{:T(128)S(6)} %add.21), channel_id=1, replica_groups=mesh['dp'=8,'mp'=4] {'dp','mp'}, use_global_device_ids=true, to_apply=%region_2.0 | all-reduce | flops 1 | bytes 8 | tf_op jit(solution)/shard_map/psum | solution.py:52
  103.5 29.9 %fusion = (f32[1024,2048]{1,0:T(8,128)}, f32[1024,2048]{1,0:T(8,128)}, f32[1024,2048]{1,0:T(8,128)}, f32[1024,2048]{1,0:T(8,128)}) fusion(f32[2048,1024]{0,1:T(8,128)} %get-tuple-element.12, f32[1024,2048]{1,0:T(8,128)} %copy-done.1, f32[]{:T(128)S(6)} %sqrt.3, f32[1024,2048]{1,0:T(8,128)} %copy-done, f32[1024,2048]{1,0:T(8,128)} %get-tuple-element.14), kind=kLoop, calls=%fused_computation.2 | loop fusion | flops 20971520 | bytes 67108864 | tf_op jit(solution)/shard_map/mul | solution.py:54
  (4 shorter events, 0.1 us)
Async XLA Ops:
  0.6 20.1 %all-to-all-start = ((bf16[4,8,1024]{2,0,1:T(4,128)(2,1)}), bf16[4,8,1024]{2,0,1:T(4,128)(2,1)S(1)}, u32[]{:S(2)}, u32[]{:S(2)}) async-start(bf16[4,8,1024]{2,0,1:T(4,128)(2,1)} %bitcast.22), calls=%async_computation | async-start | bytes 131072 | tf_op jit(solution)/shard_map/all_to_all | solution.py:40
  20.7 23.2 %all-to-all-start.1 = ((bf16[4,8,1024]{2,0,1:T(4,128)(2,1)}), bf16[4,8,1024]{2,0,1:T(4,128)(2,1)S(1)}, u32[]{:S(2)}, u32[]{:S(2)}) async-start(bf16[4,8,1024]{2,0,1:T(4,128)(2,1)} %bitcast.4), calls=%async_computation.1 | async-start | bytes 131072 | tf_op jit(solution)/shard_map/all_to_all | solution.py:44
  45.3 7.8 %copy-start = (f32[1024,2048]{1,0:T(8,128)}, f32[1024,2048]{1,0:T(8,128)S(1)}, u32[]{:S(2)}) copy-start(f32[1024,2048]{1,0:T(8,128)S(1)} %fusion.6) | copy-start | bytes 25165828
  54.3 7.7 %copy-start.1 = (f32[1024,2048]{1,0:T(8,128)}, f32[1024,2048]{1,0:T(8,128)S(1)}, u32[]{:S(2)}) copy-start(f32[1024,2048]{1,0:T(8,128)S(1)} %fusion.5) | copy-start | bytes 25165828
where the time goes:
time: 134 us; the launch traced here: 133 us
  blocking collectives  72.4 us (54%)
  other arithmetic  30.6 us (23%)
  matrix products  18 us (13%)
  starting transfers between devices  9.48 us (7%)
  between operations  2.7 us (2%)
    psum x1, blocking collectives, shards(): sq_norm = lax.psum(term_in + term_out, ('dp', 'mp'))  39.4 us
    mul x1, other arithmetic, shards(): direction_in = gradient_in / precond_in * rescale  29.9 us
    dot_general x2, matrix products, accumulate(): lax.dot_general(act_block, adj_piece, contract, preferred_element_type=jn...  15.4 us
    all_gather x1, blocking collectives, shards(): wide_hidden = lax.all_gather(hidden, 'mp', axis=1, tiled=True)  14.1 us
    all_gather x1, blocking collectives, shards(): lax.all_gather(adjoint, 'dp', axis=0, tiled=True)  9.71 us
    all_gather x1, blocking collectives, shards(): lax.all_gather(output_adjoint, 'dp', axis=0, tiled=True)  9.16 us
    all_to_all x1, starting transfers between devices, shards(): lax.all_to_all(layer_input, 'dp', split_axis=1, concat_axis=0, tiled=True)  5.21 us
    all_to_all x1, starting transfers between devices, shards(): lax.all_to_all(wide_hidden, 'dp', split_axis=1, concat_axis=0, tiled=True)  4.27 us
  transfers between devices with their start and end apart: 2, of which 0 were waited for; matrix products, arithmetic and copies ran while one was open for 1% of the time, Pallas kernels for 0%

commit v1 on v0

--- a/solution.py
+++ b/solution.py
@@ -7,6 +7,16 @@
 H = 8192
 DAMPING = 0.1
 EXPONENT = 0.75
+
+
+def turned_line(x, axis, d):
+    size = lax.axis_size(axis)
+    current, tiles = (x, [x])
+    for _ in range(size - 1):
+        current = lax.ppermute(current, axis, [(i, (i + 1) % size) for i in range(size)])
+        tiles.insert(0, current)
+    merged = jnp.concatenate(tiles, axis=d)
+    return jnp.roll(merged, (lax.axis_index(axis) + 1) * x.shape[d], axis=d)
 
 
 def square_bf(values):
@@ -40,7 +50,7 @@
     own_input = lax.all_to_all(layer_input, "dp", split_axis=1, concat_axis=0, tiled=True)
     sq_input = square_bf(own_input)
     total_rows = own_input.shape[0]
-    wide_hidden = lax.all_gather(hidden, "mp", axis=1, tiled=True)
+    wide_hidden = turned_line(hidden, "mp", 1)
     own_hidden = lax.all_to_all(wide_hidden, "dp", split_axis=1, concat_axis=0, tiled=True)
     sq_hidden = square_bf(own_hidden)
     sums_in = accumulate(own_input, sq_input, lax.all_gather(adjoint, "dp", axis=0, tiled=True))

time: 134 us -> 130 us (0.970)
  blocking collectives: 72.4 us -> 58.5 us
  local copies, waits for them, and re-layouts: 0.12 us -> 4.25 us
  starting transfers between devices: 9.48 us -> 13.4 us
  other arithmetic: 30.6 us -> 32.2 us
    all_gather x1 -> x0, blocking collectives: 14.1 us -> none  [shards(): wide_hidden = lax.all_gather(hidden, 'mp', axis=1, tiled=True)]
    ppermute x0 -> x3, starting transfers between devices: none -> 6.35 us  [turned_line(): lax.ppermute(current, axis, [(i, (i + 1) % size) for i in range(size)])]
    unnamed x6 -> x12, local copies, waits for them, and re-layouts: 0.08 us -> 3.55 us
    all_to_all x1, starting transfers between devices: 5.21 us -> 3.72 us  [shards(): lax.all_to_all(layer_input, 'dp', split_axis=1, concat_axis=0, tiled=True)]
  transfers between devices with their start and end apart: 2 -> 5, of which waited for: 0 -> 0; matrix products, arithmetic and copies ran while one was open for 1% -> 9% of each run, Pallas kernels for 0% -> 0%
where the time goes in v1:
time: 130 us; the launch traced here: 129 us
  blocking collectives  58.5 us (45%)
  other arithmetic  32.2 us (25%)
  matrix products  18 us (14%)
  starting transfers between devices  13.4 us (10%)
  local copies, waits for them, and re-layouts  4.25 us (3%)
  between operations  2.74 us (2%)
    psum x1, blocking collectives, shards(): sq_norm = lax.psum(term_in + term_out, ('dp', 'mp'))  39.7 us
    mul x1, other arithmetic, shards(): direction_in = gradient_in / precond_in * rescale  29.9 us
    dot_general x2, matrix products, accumulate(): lax.dot_general(act_block, adj_piece, contract, preferred_element_type=jn...  15.4 us
    all_gather x1, blocking collectives, shards(): lax.all_gather(adjoint, 'dp', axis=0, tiled=True)  9.65 us
    all_gather x1, blocking collectives, shards(): lax.all_gather(output_adjoint, 'dp', axis=0, tiled=True)  9.14 us
    ppermute x3, starting transfers between devices, turned_line(): lax.ppermute(current, axis, [(i, (i + 1) % size) for i in range(size)])  6.35 us
    all_to_all x1, starting transfers between devices, shards(): lax.all_to_all(layer_input, 'dp', split_axis=1, concat_axis=0, tiled=True)  3.72 us
    unnamed x12, local copies, waits for them, and re-layouts  3.55 us
  transfers between devices with their start and end apart: 5, of which 0 were waited for; matrix products, arithmetic and copies ran while one was open for 9% of the time, Pallas kernels for 0%

profile of v1, /device:TPU:0, one launch (start us, length us, event | category | flops | bytes accessed | tf_op | source)
XLA Modules:
  0.0 129.1 jit_solution(1162542685582596170)
XLA Ops:
  0.6 0.8 fusion.13
  1.4 3.1 %collective-permute-start = (bf16[4,2048]{1,0:T(4,128)(2,1)S(1)}, bf16[4,2048]{1,0:T(4,128)(2,1)S(1)}, u32[]{:S(2)}, u32[]{:S(2)}) collective-permute-start(bf16[4,2048]{1,0:T(4,128)(2,1)S(1)} %get-tuple-element.9), channel_id=1, source_target_pairs={{0,1},{1,2},{2,3},{3,0},{4,5},{5,6},{6,7},{7,4},{8,9},{9,10},{10,1... | collective-permute-start | bytes 49160 | tf_op jit(solution)/shard_map/ppermute | solution.py:16
  4.5 3.7 %all-to-all-start = ((bf16[4,8,1024]{2,0,1:T(4,128)(2,1)}), bf16[4,8,1024]{2,0,1:T(4,128)(2,1)S(1)}, u32[]{:S(2)}, u32[]{:S(2)}) async-start(bf16[4,8,1024]{2,0,1:T(4,128)(2,1)} %bitcast.22), calls=%async_computation | async-start | bytes 131072 | tf_op jit(solution)/shard_map/all_to_all | solution.py:50
  8.2 0.0 collective-permute-done
  8.3 1.6 %collective-permute-start.1 = (bf16[4,2048]{1,0:T(4,128)(2,1)S(1)}, bf16[4,2048]{1,0:T(4,128)(2,1)S(1)}, u32[]{:S(2)}, u32[]{:S(2)}) collective-permute-start(bf16[4,2048]{1,0:T(4,128)(2,1)S(1)} %collective-permute-done), channel_id=1, source_target_pairs={{0,1},{1,2},{2,3},{3,0},{4,5},{5,6},{6,7},{7,4},{8,9},{9,10},{10,1... | collective-permute-start | bytes 49160 | tf_op jit(solution)/shard_map/ppermute | solution.py:16
  9.9 9.7 %all-gather = bf16[8,4,2048]{2,1,0:T(4,128)(2,1)S(1)} all-gather(bf16[1,4,2048]{2,1,0:T(4,128)(2,1)S(1)} %get-tuple-element.10), channel_id=1, replica_groups=mesh['dp'=8,'mp'=4] {'dp'}, dimensions={0}, use_global_device_ids=true | all-gather | bytes 147456 | tf_op jit(solution)/shard_map/all_gather | solution.py:56
  19.6 0.0 collective-permute-done.1
  19.6 1.6 %collective-permute-start.2 = (bf16[4,2048]{1,0:T(4,128)(2,1)S(1)}, bf16[4,2048]{1,0:T(4,128)(2,1)S(1)}, u32[]{:S(2)}, u32[]{:S(2)}) collective-permute-start(bf16[4,2048]{1,0:T(4,128)(2,1)S(1)} %collective-permute-done.1), channel_id=1, source_target_pairs={{0,1},{1,2},{2,3},{3,0},{4,5},{5,6},{6,7},{7,4},{8,9},{9,10},{10,1... | collective-permute-start | bytes 49160 | tf_op jit(solution)/shard_map/ppermute | solution.py:16
  21.2 9.1 %all-gather.1 = bf16[8,4,2048]{2,1,0:T(4,128)(2,1)S(1)} all-gather(bf16[1,4,2048]{2,1,0:T(4,128)(2,1)} %bitcast.23), channel_id=1, replica_groups=mesh['dp'=8,'mp'=4] {'dp'}, dimensions={0}, use_global_device_ids=true | all-gather | bytes 147456 | tf_op jit(solution)/shard_map/all_gather | solution.py:58
  30.4 0.0 collective-permute-done.2
  30.5 0.8 constant_dynamic-update-slice_fusion.4
  31.3 0.8 constant_dynamic-update-slice_fusion
  32.0 0.7 constant_dynamic-slice_fusion
  32.7 0.0 all-to-all-done
  32.7 3.4 %all-to-all-start.1 = ((bf16[4,8,1024]{2,0,1:T(4,128)(2,1)}), bf16[4,8,1024]{2,0,1:T(4,128)(2,1)S(1)}, u32[]{:S(2)}, u32[]{:S(2)}) async-start(bf16[4,8,1024]{2,0,1:T(4,128)(2,1)} %bitcast.4), calls=%async_computation.1 | async-start | bytes 131072 | tf_op jit(solution)/shard_map/all_to_all | solution.py:54
  36.1 1.3 fusion.5
  37.4 0.0 copy-start
  37.4 3.4 %copy-done = f32[1024,2048]{1,0:T(8,128)} copy-done((f32[1024,2048]{1,0:T(8,128)}, f32[1024,2048]{1,0:T(8,128)S(1)}, u32[]{:S(2)}) %copy-start) | copy-done | bytes 8388632
  40.8 7.6 %fusion.2 = (f32[]{:T(128)}, f32[2048,1024]{0,1:T(8,128)}) fusion(f32[1024,2048]{1,0:T(8,128)S(1)} %fusion.5, bf16[32,2048]{1,0:T(8,128)(2,1)S(1)} %reshape.17, bf16[32,1024]{1,0:T(8,128)(2,1)S(1)} %all_to_all.31), kind=kOutput, calls=%fused_computation.4 | convolution fusion | flops 146800640 | bytes 16973828 | tf_op jit(solution)/shard_map/dot_general | solution.py:29
  48.4 0.0 all-to-all-done.1
  48.4 1.3 fusion.6
  49.7 0.0 copy-start.1
  49.7 7.8 %multiply_reduce_fusion = (f32[]{:T(128)}, f32[1024,2048]{1,0:T(8,128)}) fusion(f32[1024,2048]{1,0:T(8,128)S(1)} %fusion.6, bf16[32,1024]{1,0:T(8,128)(2,1)S(1)} %all_to_all.35, bf16[32,2048]{1,0:T(8,128)(2,1)S(1)} %reshape.19), kind=kOutput, calls=%fused_computation.6 | convolution fusion | flops 146800640 | bytes 16973828 | tf_op jit(solution)/shard_map/dot_general | solution.py:29
  57.5 0.0 copy-done.1
  58.8 39.7 %psum.7 = f32[]{:T(128)} all-reduce(f32[]{:T(128)S(6)} %add.37), channel_id=1, replica_groups=mesh['dp'=8,'mp'=4] {'dp','mp'}, use_global_device_ids=true, to_apply=%region_2.3 | all-reduce | flops 1 | bytes 8 | tf_op jit(solution)/shard_map/psum | solution.py:62
  99.2 29.9 %fusion = (f32[1024,2048]{1,0:T(8,128)}, f32[1024,2048]{1,0:T(8,128)}, f32[1024,2048]{1,0:T(8,128)}, f32[1024,2048]{1,0:T(8,128)}) fusion(f32[2048,1024]{0,1:T(8,128)} %get-tuple-element.12, f32[1024,2048]{1,0:T(8,128)} %copy-done, f32[]{:T(128)S(6)} %sqrt.3, f32[1024,2048]{1,0:T(8,128)} %copy-done.1, f32[1024,2048]{1,0:T(8,128)} %get-tuple-element.14), kind=kLoop, calls=%fused_computation.2 | loop fusion | flops 20971520 | bytes 67108864 | tf_op jit(solution)/shard_map/mul | solution.py:64
  (10 shorter events, 0.2 us)
Async XLA Ops:
  1.4 6.8 %collective-permute-start = (bf16[4,2048]{1,0:T(4,128)(2,1)S(1)}, bf16[4,2048]{1,0:T(4,128)(2,1)S(1)}, u32[]{:S(2)}, u32[]{:S(2)}) collective-permute-start(bf16[4,2048]{1,0:T(4,128)(2,1)S(1)} %get-tuple-element.9), channel_id=1, source_target_pairs={{0,1},{1,2},{2,3},{3,0},{4,5},{5,6},{6,7},{7,4},{8,9},{9,10},{10,1... | collective-permute-start | bytes 49160 | tf_op jit(solution)/shard_map/ppermute | solution.py:16
  4.5 28.2 %all-to-all-start = ((bf16[4,8,1024]{2,0,1:T(4,128)(2,1)}), bf16[4,8,1024]{2,0,1:T(4,128)(2,1)S(1)}, u32[]{:S(2)}, u32[]{:S(2)}) async-start(bf16[4,8,1024]{2,0,1:T(4,128)(2,1)} %bitcast.22), calls=%async_computation | async-start | bytes 131072 | tf_op jit(solution)/shard_map/all_to_all | solution.py:50
  8.3 11.3 %collective-permute-start.1 = (bf16[4,2048]{1,0:T(4,128)(2,1)S(1)}, bf16[4,2048]{1,0:T(4,128)(2,1)S(1)}, u32[]{:S(2)}, u32[]{:S(2)}) collective-permute-start(bf16[4,2048]{1,0:T(4,128)(2,1)S(1)} %collective-permute-done), channel_id=1, source_target_pairs={{0,1},{1,2},{2,3},{3,0},{4,5},{5,6},{6,7},{7,4},{8,9},{9,10},{10,1... | collective-permute-start | bytes 49160 | tf_op jit(solution)/shard_map/ppermute | solution.py:16
  19.6 10.8 %collective-permute-start.2 = (bf16[4,2048]{1,0:T(4,128)(2,1)S(1)}, bf16[4,2048]{1,0:T(4,128)(2,1)S(1)}, u32[]{:S(2)}, u32[]{:S(2)}) collective-permute-start(bf16[4,2048]{1,0:T(4,128)(2,1)S(1)} %collective-permute-done.1), channel_id=1, source_target_pairs={{0,1},{1,2},{2,3},{3,0},{4,5},{5,6},{6,7},{7,4},{8,9},{9,10},{10,1... | collective-permute-start | bytes 49160 | tf_op jit(solution)/shard_map/ppermute | solution.py:16
  32.7 15.7 %all-to-all-start.1 = ((bf16[4,8,1024]{2,0,1:T(4,128)(2,1)}), bf16[4,8,1024]{2,0,1:T(4,128)(2,1)S(1)}, u32[]{:S(2)}, u32[]{:S(2)}) async-start(bf16[4,8,1024]{2,0,1:T(4,128)(2,1)} %bitcast.4), calls=%async_computation.1 | async-start | bytes 131072 | tf_op jit(solution)/shard_map/all_to_all | solution.py:54
  37.4 3.4 %copy-start = (f32[1024,2048]{1,0:T(8,128)}, f32[1024,2048]{1,0:T(8,128)S(1)}, u32[]{:S(2)}) copy-start(f32[1024,2048]{1,0:T(8,128)S(1)} %fusion.5) | copy-start | bytes 25165828
  49.7 7.8 %copy-start.1 = (f32[1024,2048]{1,0:T(8,128)}, f32[1024,2048]{1,0:T(8,128)S(1)}, u32[]{:S(2)}) copy-start(f32[1024,2048]{1,0:T(8,128)S(1)} %fusion.6) | copy-start | bytes 25165828
